TPU v7x, 32 devices: a whole 2x2x4 slice. The times are simulated.
32 devices in a mesh: subset: 8 (over z, x), vocab: 4 (over y, core).
Axes of the slice: x: 2, y: 2, z: 4, core: 2. Of those that a mesh axis runs over, the one named last changes fastest.
Arguments:
- hidden: bfloat16 [4096, 2048], P('subset', 'vocab'), may hold values from -100 to 100
- proj_weight: bfloat16 [2048, 25600], P('subset', 'vocab'), may hold values from -1 to 1
- targets: int32 [4096], P('subset'), may hold values from 0 to 25599
- counts: int32 [8, 100, 512], P('subset', 'vocab'), may hold values from 1 to 15, as said below
- ranks: int32 [8], replicated, may hold values from 0 to 799
Outputs:
- row_cross_entropy: float32 [4096], P('subset')
- resample_mean_losses: float32 [8, 100], P('subset', 'vocab')
- quantiles: float32 [8], replicated
Inputs may be any that keep to these rules, and one draw needn't show every extreme that they name: For every subset and resample the counts over the 512 rows sum to 4096.
All inputs are finite; a program needn't handle non-finite values.
Results may differ from a plain program's by a relative error of at most 0.0003.
Values may be sent and summed in bfloat16 or wider, within the bound.
No kernel may reach another device: no remote copies, remote signals or barrier semaphores. Data moves between devices by JAX's collectives and lax.ppermute only.
A program may use at most 128 MiB of HBM per device.

v0:
```python
import jax
import jax.numpy as jnp
from jax import lax
from jax.sharding import PartitionSpec as P


def shards(hidden, proj_weight, targets, counts, ranks):
    features = lax.all_gather(hidden, "vocab", axis=1, tiled=True)
    columns = proj_weight.shape[1]
    whole_weight = lax.all_gather(proj_weight, "subset", axis=0, tiled=True)
    logit_scores = jnp.dot(features, whole_weight, preferred_element_type=jnp.float32)
    local_top = jnp.max(logit_scores, axis=1)
    local_sum = jnp.sum(jnp.exp(logit_scores - local_top[:, None]), axis=1)
    offset = targets - lax.axis_index("vocab") * columns
    inside = (offset >= 0) & (offset < columns)
    picked = jnp.take_along_axis(logit_scores, jnp.clip(offset, 0, columns - 1)[:, None], axis=1)[
        :, 0
    ]
    picked = jnp.where(inside, picked, 0.0)
    row_max = lax.pmax(local_top, "vocab")
    row_total, target_logit = lax.psum((local_sum * jnp.exp(local_top - row_max), picked), "vocab")
    row_cross_entropy = row_max + jnp.log(row_total) - target_logit
    total_rows = 1.0 * lax.axis_size("subset") * row_cross_entropy.shape[0]
    resample_mean_losses = (
        jnp.einsum(
            "cno,o->cn",
            counts.astype(jnp.float32),
            row_cross_entropy,
            precision=lax.Precision.HIGHEST,
        )
        / total_rows
    )
    grouped = lax.all_gather(resample_mean_losses, "vocab", axis=1, tiled=True)
    gathered = lax.all_gather(grouped, "subset", axis=0, tiled=True)
    pooled = jnp.sort(gathered.reshape(-1))
    positions = lax.iota(jnp.int32, pooled.shape[0])
    chosen = positions[:, None] == ranks[None, :]
    quantiles = jnp.sum(jnp.where(chosen, pooled[:, None], 0.0), axis=0)
    return (row_cross_entropy, resample_mean_losses, quantiles)


def solution(mesh):
    return jax.shard_map(
        shards,
        mesh=mesh,
        in_specs=(
            P("subset", "vocab"),
            P("subset", "vocab"),
            P("subset"),
            P("subset", "vocab", None),
            P(),
        ),
        out_specs=(P("subset"), P("subset", "vocab"), P()),
        check_vma=False,
    )
```

profile of v0, /device:TPU:0, one launch (start us, length us, event | category | flops | bytes accessed | tf_op | source)
XLA Modules:
  0.0 625.1 jit_solution(13795552494358012324)
XLA Ops:
  7.2 0.0 all-gather.5.cloned.1.call-start
  7.2 0.7 all-gather.5.cloned.1.call-update
  7.9 0.0 all-gather.7.cloned.1.call-start
  7.9 0.7 all-gather.7.cloned.1.call-update
  8.7 0.8 convert_element_type.3
  9.5 1.2 dynamic-slice
  10.8 1.2 dynamic-slice.1
  13.3 0.7 compare_select_fusion
  14.0 20.8 %all-gather.5.cloned.1.call-done = bf16[512,2048]{1,0:T(8,128)(2,1)} async-done(((bf16[512,512]{1,0:T(8,128)(2,1)}), bf16[512,2048]{1,0:T(8,128)(2,1)}) %all-gather.5.cloned.1.call-update) | async-done | bytes 2097168 | tf_op jit(solution)/shard_map/all_gather | solution.py:8
  34.9 501.6 %all-gather.7.cloned.1.call-done = bf16[2048,6400]{1,0:T(8,128)(2,1)} async-done(((bf16[256,6400]{1,0:T(8,128)(2,1)}), bf16[2048,6400]{1,0:T(8,128)(2,1)}) %all-gather.7.cloned.1.call-update) | async-done | bytes 26214416 | tf_op jit(solution)/shard_map/all_gather | solution.py:10
  536.4 22.5 %fusion.6 = (f32[512]{0:T(512)S(1)}, f32[512,6400]{1,0:T(8,128)}) fusion(bf16[512,2048]{1,0:T(8,128)(2,1)} %all-gather.5.cloned.1.call-done, bf16[2048,6400]{1,0:T(8,128)(2,1)} %all-gather.7.cloned.1.call-done), kind=kOutput, calls=%fused_computation.18 | convolution fusion | flops 13425049600 | bytes 41420800 | tf_op jit(solution)/shard_map/dot_general | solution.py:11
  558.9 0.0 copy-start
  558.9 0.0 copy-start.3
  558.9 6.5 %pmax.7 = f32[512]{0:T(512)S(1)} all-reduce(f32[512]{0:T(512)S(1)} %get-tuple-element.8), channel_id=1, replica_groups=mesh['subset'=8,'vocab'=4] {'vocab'}, use_global_device_ids=true, to_apply=%region_1.0 | all-reduce | flops 512 | bytes 4096 | tf_op jit(solution)/shard_map/pmax | solution.py:20
  565.5 6.6 %exponential_reduce_fusion = f32[512]{0:T(512)S(1)} fusion(f32[512,6400]{1,0:T(8,128)} %get-tuple-element.9, f32[512]{0:T(512)S(1)} %get-tuple-element.8), kind=kLoop, calls=%fused_computation.1 | loop fusion | flops 6553088 | bytes 13111296 | tf_op jit(solution)/shard_map/reduce_sum | solution.py:13
  572.0 8.2 %gather_fusion = f32[512]{0:T(512)S(1)} fusion(f32[512,6400]{1,0:T(8,128)} %get-tuple-element.9, s32[512]{0:T(512)S(1)} %bitcast.18), kind=kCustom, calls=%fused_computation | custom fusion | bytes 8192 | tf_op jit(solution)/shard_map/jit(take_along_axis)/gather | solution.py:16
  580.2 0.0 copy-done
  580.2 5.8 all-reduce.2
  586.1 0.0 copy-start.1
  586.1 0.1 fusion
  586.2 0.0 copy-start.2
  586.3 0.2 dynamic-update-slice
  586.5 5.7 all-reduce
  592.3 0.2 dynamic-update-slice.1
  592.5 20.5 %all-reduce.1 = f32[800]{0:T(1024)S(1)} all-reduce(f32[800]{0:T(1024)S(1)} %dynamic-update-slice.1), channel_id=3, replica_groups=mesh['subset'=8,'vocab'=4] {'subset'}, use_global_device_ids=true, to_apply=%add.1 | all-reduce | flops 800 | bytes 6400
  613.0 4.5 sort.15
  617.5 0.0 copy-done.3
  617.6 0.7 select_reduce_fusion
  618.3 0.0 copy-done.1
  618.3 0.0 copy-done.2
  (9 shorter events, 0.1 us)
Async XLA Ops:
  7.2 27.7 %all-gather.5.cloned.1.call-start = ((), (), s32[]{:S(2)}) async-start(), calls=%async_computation | async-start | bytes 2621440 | tf_op jit(solution)/shard_map/all_gather | solution.py:8
  7.9 528.6 %all-gather.7.cloned.1.call-start = ((), (), s32[]{:S(2)}) async-start(), calls=%async_computation.1 | async-start | bytes 29491200 | tf_op jit(solution)/shard_map/all_gather | solution.py:10
  558.9 21.3 %copy-start = (s32[512]{0:T(512)S(1)}, s32[512]{0:T(512)}, u32[]{:S(2)}) copy-start(s32[512]{0:T(512)} %param.7) | copy-start | bytes 6148
  558.9 58.6 %copy-start.3 = (s32[8]{0:T(128)S(1)}, s32[8]{0:T(128)}, u32[]{:S(2)}) copy-start(s32[8]{0:T(128)} %param.9) | copy-start | bytes 100
  586.1 32.2 %copy-start.1 = (f32[512]{0:T(512)}, f32[512]{0:T(512)S(1)}, u32[]{:S(2)}) copy-start(f32[512]{0:T(512)S(1)} %add_subtract_fusion) | copy-start | bytes 6148
  586.2 32.0 %copy-start.2 = (f32[25]{0:T(128)}, f32[25]{0:T(128)S(1)}, u32[]{:S(2)}) copy-start(f32[25]{0:T(128)S(1)} %fusion) | copy-start | bytes 304
Sparse Core Ops, SparseCore 0:
  9.5 25.2 all-gather.4
  36.4 500.0 all-gather.6
where the time goes:
time: 626 us; the launch traced here: 625 us
  waiting for transfers between devices  524 us (84%)
  blocking collectives  38.6 us (6%)
  matrix products  22.6 us (4%)
  between operations  15.4 us (2%)
  other arithmetic  13.4 us (2%)
  local copies, waits for them, and re-layouts  11.1 us (2%)
    all_gather x1, waiting for transfers between devices, shards(): whole_weight = lax.all_gather(proj_weight, 'subset', axis=0, tiled=True)  502 us
    unnamed x2, blocking collectives  26.3 us
    dot_general x1, matrix products, shards(): jnp.dot(features, whole_weight, preferred_element_type=jnp.float32)  22.5 us
    all_gather x1, waiting for transfers between devices, shards(): features = lax.all_gather(hidden, 'vocab', axis=1, tiled=True)  20.8 us
  transfers between devices with their start and end apart: 2, of which 2 were waited for; matrix products, arithmetic and copies ran while one was open for 1% of the time, Pallas kernels for 0%

commit v1 on v0

--- a/solution.py
+++ b/solution.py
@@ -7,7 +7,8 @@
 def shards(hidden, proj_weight, targets, counts, ranks):
     features = lax.all_gather(hidden, "vocab", axis=1, tiled=True)
     columns = proj_weight.shape[1]
-    whole_weight = lax.all_gather(proj_weight, "subset", axis=0, tiled=True)
+    sent = jnp.stack([proj_weight] * lax.axis_size("subset"))
+    whole_weight = jnp.concatenate(lax.all_to_all(sent, "subset", 0, 0), axis=0)
     logit_scores = jnp.dot(features, whole_weight, preferred_element_type=jnp.float32)
     local_top = jnp.max(logit_scores, axis=1)
     local_sum = jnp.sum(jnp.exp(logit_scores - local_top[:, None]), axis=1)

time: 626 us -> 679 us (1.085)
  waiting for transfers between devices: 524 us -> 564 us
  local copies, waits for them, and re-layouts: 11.1 us -> 19.7 us
  starting transfers between devices: 0.08 us -> 7.46 us
    all_to_all x0 -> x1, waiting for transfers between devices: none -> 540 us  [shards(): whole_weight = jnp.concatenate(lax.all_to_all(sent, 'subset', 0, 0), axis=0)]
    all_gather x1 -> x0, waiting for transfers between devices: 502 us -> none  [shards(): whole_weight = lax.all_gather(proj_weight, 'subset', axis=0, tiled=True)]
    another operation x1 -> x2, local copies, waits for them, and re-layouts: 0.01 us -> 9.85 us  [the longest x1 9.85 us: shards(): sent = jnp.stack([proj_weight] * lax.axis_size('subset'))]
    all_to_all x0 -> x1, starting transfers between devices: none -> 7.42 us  [shards(): whole_weight = jnp.concatenate(lax.all_to_all(sent, 'subset', 0, 0), axis=0)]
  transfers between devices with their start and end apart: 2 -> 2, of which waited for: 2 -> 2; matrix products, arithmetic and copies ran while one was open for 1% -> 0% of each run, Pallas kernels for 0% -> 0%
where the time goes in v1:
time: 679 us; the launch traced here: 678 us
  waiting for transfers between devices  564 us (83%)
  blocking collectives  37.1 us (5%)
  matrix products  22.6 us (3%)
  local copies, waits for them, and re-layouts  19.7 us (3%)
  between operations  15.5 us (2%)
  other arithmetic  11.9 us (2%)
  starting transfers between devices  7.46 us (1%)
    all_to_all x1, waiting for transfers between devices, shards(): whole_weight = jnp.concatenate(lax.all_to_all(sent, 'subset', 0, 0), axis=0)  540 us
    unnamed x2, blocking collectives  25.3 us
    all_gather x1, waiting for transfers between devices, shards(): features = lax.all_gather(hidden, 'vocab', axis=1, tiled=True)  23.7 us
    dot_general x1, matrix products, shards(): jnp.dot(features, whole_weight, preferred_element_type=jnp.float32)  22.5 us
  transfers between devices with their start and end apart: 2, of which 2 were waited for; matrix products, arithmetic and copies ran while one was open for 0% of the time, Pallas kernels for 0%

profile of v1, /device:TPU:0, one launch (start us, length us, event | category | flops | bytes accessed | tf_op | source)
XLA Modules:
  0.0 678.1 jit_solution(13325294804173188870)
XLA Ops:
  7.2 9.8 %stack.2 = bf16[8,256,6400]{2,1,0:T(8,128)(2,1)} broadcast(bf16[256,6400]{1,0:T(8,128)(2,1)} %param.6), dimensions={1,2} | broadcast | bytes 29491200 | tf_op jit(solution)/shard_map/stack | solution.py:10
  17.0 0.0 copy-start
  17.0 0.0 copy-start.6
  17.0 0.0 copy-start.5
  17.0 0.0 copy-start.1
  17.0 7.4 %all-to-all-start = ((bf16[8,256,6400]{2,1,0:T(8,128)(2,1)}), bf16[8,256,6400]{2,1,0:T(8,128)(2,1)}, u32[]{:S(2)}, u32[]{:S(2)}) async-start(bf16[8,256,6400]{2,1,0:T(8,128)(2,1)} %stack.2), calls=%async_computation | async-start | bytes 52428800 | tf_op jit(solution)/shard_map/all_to_all | solution.py:11
  24.5 0.0 all-gather.4.cloned.1.call-start
  24.5 0.7 all-gather.4.cloned.1.call-update
  25.2 0.0 copy-done
  25.3 0.0 copy-done.6
  25.3 0.6 dynamic-slice
  25.9 0.0 copy-done.5
  25.9 0.6 dynamic-slice.1
  27.8 0.0 copy-done.1
  27.8 23.7 %all-gather.4.cloned.1.call-done = bf16[512,2048]{1,0:T(8,128)(2,1)} async-done(((bf16[512,512]{1,0:T(8,128)(2,1)}), bf16[512,2048]{1,0:T(8,128)(2,1)}) %all-gather.4.cloned.1.call-update) | async-done | bytes 2097168 | tf_op jit(solution)/shard_map/all_gather | solution.py:8
  51.5 539.5 %all-to-all-done = bf16[8,256,6400]{2,1,0:T(8,128)(2,1)} async-done(((bf16[8,256,6400]{2,1,0:T(8,128)(2,1)}), bf16[8,256,6400]{2,1,0:T(8,128)(2,1)}, u32[]{:S(2)}, u32[]{:S(2)}) %all-to-all-start) | async-done | bytes 26214432 | tf_op jit(solution)/shard_map/all_to_all | solution.py:11
  591.0 22.5 %fusion.6 = (f32[512]{0:T(512)S(1)}, f32[512,6400]{1,0:T(8,128)}) fusion(bf16[512,2048]{1,0:T(8,128)(2,1)} %all-gather.4.cloned.1.call-done, bf16[2048,6400]{1,0:T(8,128)(2,1)} %bitcast), kind=kOutput, calls=%fused_computation.18 | convolution fusion | flops 13425049600 | bytes 41420800 | tf_op jit(solution)/shard_map/dot_general | solution.py:12
  613.5 0.0 copy-start.4
  613.5 5.6 pmax.7
  619.2 6.6 exponential_reduce_fusion
  625.7 8.2 %gather_fusion = f32[512]{0:T(512)S(1)} fusion(f32[512,6400]{1,0:T(8,128)} %get-tuple-element.9, s32[512]{0:T(512)S(1)} %bitcast.19), kind=kCustom, calls=%fused_computation | custom fusion | bytes 8192 | tf_op jit(solution)/shard_map/jit(take_along_axis)/gather | solution.py:17
  633.9 6.1 all-reduce.2
  640.1 0.0 copy-start.2
  640.1 0.1 fusion
  640.2 0.0 copy-start.3
  640.2 0.2 dynamic-update-slice
  640.5 5.8 all-reduce
  646.3 0.2 dynamic-update-slice.1
  646.5 19.5 %all-reduce.1 = f32[800]{0:T(1024)S(1)} all-reduce(f32[800]{0:T(1024)S(1)} %dynamic-update-slice.1), channel_id=3, replica_groups=mesh['subset'=8,'vocab'=4] {'subset'}, use_global_device_ids=true, to_apply=%add.1 | all-reduce | flops 800 | bytes 6400
  666.0 4.5 sort.15
  670.6 0.0 copy-done.4
  670.6 0.7 select_reduce_fusion
  671.3 0.0 copy-done.2
  671.3 0.0 copy-done.3
  (11 shorter events, 0.1 us)
Async XLA Ops:
  17.0 8.2 %copy-start = (s32[1,25,512]{2,0,1:T(1,128)S(1)}, s32[1,25,512]{2,0,1:T(1,128)}, u32[]{:S(2)}) copy-start(s32[1,25,512]{2,0,1:T(1,128)} %param.8) | copy-start | bytes 153604
  17.0 8.3 %copy-start.6 = (u32[32]{0:T(128)S(1)}, u32[32]{0:T(128)}, u32[]{:S(2)}) copy-start(u32[32]{0:T(128)} %constant.61) | copy-start | bytes 388
  17.0 8.9 %copy-start.5 = (u32[32]{0:T(128)S(1)}, u32[32]{0:T(128)}, u32[]{:S(2)}) copy-start(u32[32]{0:T(128)} %constant.66) | copy-start | bytes 388
  17.0 10.7 %copy-start.1 = (s32[512]{0:T(512)S(1)}, s32[512]{0:T(512)}, u32[]{:S(2)}) copy-start(s32[512]{0:T(512)} %param.7) | copy-start | bytes 6148
  17.0 574.0 %all-to-all-start = ((bf16[8,256,6400]{2,1,0:T(8,128)(2,1)}), bf16[8,256,6400]{2,1,0:T(8,128)(2,1)}, u32[]{:S(2)}, u32[]{:S(2)}) async-start(bf16[8,256,6400]{2,1,0:T(8,128)(2,1)} %stack.2), calls=%async_computation | async-start | bytes 52428800 | tf_op jit(solution)/shard_map/all_to_all | solution.py:11
  24.5 27.0 %all-gather.4.cloned.1.call-start = ((), (), s32[]{:S(2)}) async-start(), calls=%async_computation.1 | async-start | bytes 2621440 | tf_op jit(solution)/shard_map/all_gather | solution.py:8
  613.5 57.0 %copy-start.4 = (s32[8]{0:T(128)S(1)}, s32[8]{0:T(128)}, u32[]{:S(2)}) copy-start(s32[8]{0:T(128)} %param.9) | copy-start | bytes 100
  640.1 31.2 %copy-start.2 = (f32[512]{0:T(512)}, f32[512]{0:T(512)S(1)}, u32[]{:S(2)}) copy-start(f32[512]{0:T(512)S(1)} %add_subtract_fusion) | copy-start | bytes 6148
  640.2 31.1 %copy-start.3 = (f32[25]{0:T(128)}, f32[25]{0:T(128)S(1)}, u32[]{:S(2)}) copy-start(f32[25]{0:T(128)S(1)} %fusion) | copy-start | bytes 304
Sparse Core Ops, SparseCore 0:
  26.8 24.5 all-gather.3
